TPU v7x, 32 devices: a whole 2x2x4 slice. The times are simulated.
32 devices in a mesh: row: 4 (over x, core), col: 8 (over z, y).
Axes of the slice: x: 2, y: 2, z: 4, core: 2. Of those that a mesh axis runs over, the one named last changes fastest.
Arguments:
- matrix: float32 [3072, 12, 4096], P('row', None, 'col'), may hold values from -6 to 6
- factor: float32 [12, 4096, 2048], P(None, 'col', 'row'), as said below
Outputs:
- updated: float32 [3072, 12, 4096], P('row', None, 'col')
- solved: float32 [3072, 2048], P('row')
Inputs may be any that keep to these rules, and one draw needn't show every extreme that they name: factor is lower trapezoidal: zero wherever the column index exceeds the row index; its diagonal entries lie in 1 to 2.
All inputs are finite; a program needn't handle non-finite values.
Results may differ from a plain program's by a relative error of at most 0.00013.
Values sent between devices are 32-bit elements; how exact they have to be, the bound alone decides.
A program may use at most 256 MiB of HBM per device.

v0:
```python
import jax
import jax.numpy as jnp
from jax import lax
from jax.sharding import PartitionSpec as P

P_SIZE = 4


def from_root(value, axis, source):
    kept = jnp.where(lax.axis_index(axis) == source, value, 0).astype(value.dtype)
    return lax.psum(kept, axis)


def local(matrix, factor):
    col_count = lax.axis_size("col")
    col_index = lax.axis_index("col")
    nlocal = matrix.shape[1]
    block_width = matrix.shape[2]
    block_ids = jnp.arange(nlocal, dtype=jnp.int32) * col_count + col_index
    unit_block = jnp.eye(block_width, dtype=jnp.float32)
    panels = []
    columns = lax.all_gather(factor, "row", axis=2, tiled=True)
    current = matrix
    for step in range(P_SIZE):
        local_block = step // col_count
        part_cols = columns[:, :, step * block_width : (step + 1) * block_width]
        root_col = step % col_count
        guarded = jnp.where(col_index == root_col, part_cols[local_block], unit_block)
        solved_block = lax.linalg.triangular_solve(
            guarded, current[:, local_block, :], left_side=False, lower=True, transpose_a=True
        )
        solved_block = from_root(solved_block, "col", root_col)
        panels.append(solved_block)
        product_term = jnp.einsum(
            "ms,lts->mlt", solved_block, part_cols, precision=lax.Precision.HIGHEST
        )
        later_block = (block_ids > step)[None, :, None]
        current = jnp.where(later_block, current - product_term, current)
    solved = jnp.concatenate(panels, axis=1)
    return (current, solved)


def solution(mesh):
    return jax.shard_map(
        local,
        mesh=mesh,
        in_specs=(P("row", None, "col"), P(None, "col", "row")),
        out_specs=(P("row", None, "col"), P("row", None)),
        check_vma=False,
    )
```

profile of v0, /device:TPU:0, one launch (start us, length us, event | category | flops | bytes accessed | tf_op | source)
XLA Modules:
  0.0 1054.0 jit_solution(15892614803361657785)
XLA Ops:
  8.0 1.5 slice_bitcast_fusion.3
  9.5 299.9 %all-gather.2.cloned.1.call-done = f32[12,512,2048]{2,1,0:T(8,128)} async-done(((f32[12,512,512]{2,1,0:T(8,128)}), f32[12,512,2048]{2,1,0:T(8,128)}) %all-gather.2.cloned.1.call-update) | async-done | bytes 50331664 | tf_op jit(solution)/shard_map/all_gather | solution.py:22
  309.4 4.2 fusion.43
  313.6 11.5 %while.8 = (s32[]{:T(128)}, f32[512,512]{1,0:T(8,128)}, s32[4,2]{0,1:T(2,128)S(1)}, f32[4,128,128]{2,1,0:T(8,128)S(1)}, s32[]{:T(128)}) while((s32[]{:T(128)}, f32[512,512]{1,0:T(8,128)}, s32[4,2]{0,1:T(2,128)S(1)}, f32[4,128,128]{2,1,0:T(8,128)S(1)}, s32[]{:T(128)}) %tuple.71), condition=%wide.while_cond, body=%wide.while_body.sunk | while | flops 2 | bytes 131189 | solution.py:29
  314.3 2.2 bitcast_dynamic-update-slice_fusion.8
  317.1 2.2 bitcast_dynamic-update-slice_fusion.8
  320.0 2.2 bitcast_dynamic-update-slice_fusion.8
  322.9 2.1 bitcast_dynamic-update-slice_fusion.8
  325.1 39.3 %custom-call.6 = f32[4,128,128]{1,2,0:T(8,128)S(1)} custom-call(f32[4,128,128]{2,1,0:T(8,128)S(1)} %get-tuple-element.29), custom_call_target="InvertDiagBlocksLowerTriangular" | custom-call | tf_op jit(solution)/shard_map/triangular_solve/custom-call.1 | solution.py:29
  364.9 1.6 convolution_subtract_fusion.7
  367.1 2.3 convolution_subtract_fusion.11
  370.0 3.1 convolution_subtract_fusion.6
  374.9 11.5 %while.9 = (s32[]{:T(128)}, f32[512,512]{1,0:T(8,128)}, s32[4,2]{0,1:T(2,128)S(1)}, f32[4,128,128]{2,1,0:T(8,128)S(1)}, s32[]{:T(128)}) while((s32[]{:T(128)}, f32[512,512]{1,0:T(8,128)}, s32[4,2]{0,1:T(2,128)S(1)}, f32[4,128,128]{2,1,0:T(8,128)S(1)}, s32[]{:T(128)}) %tuple.93), condition=%wide.while_cond.clone, body=%wide.while_body.clone.sunk | while | flops 2 | bytes 131189 | solution.py:29
  375.6 2.2 bitcast_dynamic-update-slice_fusion.9
  378.5 2.3 bitcast_dynamic-update-slice_fusion.9
  381.4 2.2 bitcast_dynamic-update-slice_fusion.9
  384.3 2.1 bitcast_dynamic-update-slice_fusion.9
  386.5 39.3 %custom-call.7 = f32[4,128,128]{1,2,0:T(8,128)S(1)} custom-call(f32[4,128,128]{2,1,0:T(8,128)S(1)} %get-tuple-element.30), custom_call_target="InvertDiagBlocksLowerTriangular" | custom-call | tf_op jit(solution)/shard_map/triangular_solve/custom-call.1 | solution.py:29
  425.8 38.7 %all-reduce.5.cloned.1.call-done = f32[768,512]{0,1:T(8,128)} async-done(((f32[768,512]{0,1:T(8,128)}), f32[768,512]{0,1:T(8,128)}) %all-reduce.5.cloned.1.call-update) | async-done | bytes 1572880 | tf_op jit(solution)/shard_map/psum | solution.py:11
  464.5 68.7 %subtract_select_fusion.3 = f32[768,12,512]{2,0,1:T(8,128)S(1)} fusion(f32[768,12,512]{2,0,1:T(8,128)} %param.4, pred[12]{0:T(512)(128)(4,1)S(1)} %broadcast_compare_fusion, f32[12,512,2048]{2,1,0:T(8,128)} %all-gather.2.cloned.1.call-done, f32[768,512]{0,1:T(8,128)} %all-reduce.5.cloned.1.call-done), kind=kOutput, calls=%fused_computation.11 | convolution fusion | flops 29000466432 | bytes 51904524 | tf_op jit(solution)/shard_map/ms,lts->mlt/dot_general | solution.py:34
  533.8 1.7 convolution_subtract_fusion.5
  536.1 2.5 convolution_subtract_fusion.10
  539.1 3.3 convolution_subtract_fusion.4
  544.3 11.9 %while.10 = (s32[]{:T(128)}, f32[512,512]{1,0:T(8,128)}, s32[4,2]{0,1:T(2,128)S(1)}, f32[4,128,128]{2,1,0:T(8,128)S(1)}, s32[]{:T(128)}) while((s32[]{:T(128)}, f32[512,512]{1,0:T(8,128)}, s32[4,2]{0,1:T(2,128)S(1)}, f32[4,128,128]{2,1,0:T(8,128)S(1)}, s32[]{:T(128)}) %tuple.94), condition=%wide.while_cond.clone.1, body=%wide.while_body.clone.1.sunk | while | flops 2 | bytes 131189 | solution.py:29
  545.0 2.3 bitcast_dynamic-update-slice_fusion.10
  548.0 2.3 bitcast_dynamic-update-slice_fusion.10
  551.0 2.3 bitcast_dynamic-update-slice_fusion.10
  553.9 2.2 bitcast_dynamic-update-slice_fusion.10
  556.2 39.3 %custom-call.8 = f32[4,128,128]{1,2,0:T(8,128)S(1)} custom-call(f32[4,128,128]{2,1,0:T(8,128)S(1)} %get-tuple-element.31), custom_call_target="InvertDiagBlocksLowerTriangular" | custom-call | tf_op jit(solution)/shard_map/triangular_solve/custom-call.1 | solution.py:29
  595.5 37.6 %all-reduce.7.cloned.1.call-done = f32[768,512]{0,1:T(8,128)} async-done(((f32[768,512]{0,1:T(8,128)}), f32[768,512]{0,1:T(8,128)}) %all-reduce.7.cloned.1.call-update) | async-done | bytes 1572880 | tf_op jit(solution)/shard_map/psum | solution.py:11
  633.1 68.9 %subtract_select_fusion.2 = f32[768,12,512]{2,0,1:T(8,128)S(1)} fusion(f32[768,12,512]{2,0,1:T(8,128)} %copy-done.1, pred[12]{0:T(512)(128)(4,1)S(1)} %broadcast_compare_fusion.1, f32[12,512,2048]{2,1,0:T(8,128)} %all-gather.2.cloned.1.call-done, f32[768,512]{0,1:T(8,128)} %all-reduce.7.cloned.1.call-done), kind=kOutput, calls=%fused_computation.10 | convolution fusion | flops 29000466432 | bytes 51904524 | tf_op jit(solution)/shard_map/ms,lts->mlt/dot_general | solution.py:34
  702.7 1.7 convolution_subtract_fusion.3
  705.0 2.5 convolution_subtract_fusion.9
  708.0 3.3 convolution_subtract_fusion.2
  713.2 8.2 while.11
  713.8 1.4 bitcast_dynamic-update-slice_fusion.11
  715.9 1.4 bitcast_dynamic-update-slice_fusion.11
  718.0 1.4 bitcast_dynamic-update-slice_fusion.11
  720.0 1.4 bitcast_dynamic-update-slice_fusion.11
  721.4 39.3 %custom-call.9 = f32[4,128,128]{1,2,0:T(8,128)S(1)} custom-call(f32[4,128,128]{2,1,0:T(8,128)S(1)} %get-tuple-element.32), custom_call_target="InvertDiagBlocksLowerTriangular" | custom-call | tf_op jit(solution)/shard_map/triangular_solve/custom-call.1 | solution.py:29
  760.7 41.0 %all-reduce.9.cloned.1.call-done = f32[768,512]{0,1:T(8,128)} async-done(((f32[768,512]{0,1:T(8,128)}), f32[768,512]{0,1:T(8,128)}) %all-reduce.9.cloned.1.call-update) | async-done | bytes 1572880 | tf_op jit(solution)/shard_map/psum | solution.py:11
  801.7 68.9 %subtract_select_fusion.1 = f32[768,12,512]{2,0,1:T(8,128)S(1)} fusion(f32[768,12,512]{2,0,1:T(8,128)} %copy-done, pred[12]{0:T(512)(128)(4,1)S(1)} %broadcast_compare_fusion.2, f32[12,512,2048]{2,1,0:T(8,128)} %all-gather.2.cloned.1.call-done, f32[768,512]{0,1:T(8,128)} %all-reduce.9.cloned.1.call-done), kind=kOutput, calls=%fused_computation.9 | convolution fusion | flops 29000466432 | bytes 51904524 | tf_op jit(solution)/shard_map/ms,lts->mlt/dot_general | solution.py:34
  872.7 1.4 convolution_subtract_fusion.8
  874.6 2.1 convolution_subtract_fusion
  879.3 88.6 %all-reduce.11.cloned.1.call-done = f32[768,512]{0,1:T(8,128)} async-done(((f32[768,512]{0,1:T(8,128)}), f32[768,512]{0,1:T(8,128)}) %all-reduce.11.cloned.1.call-update) | async-done | bytes 1572880 | tf_op jit(solution)/shard_map/psum | solution.py:11
  967.9 5.0 pad_maximum_fusion
  973.0 6.7 copy.8
  979.6 67.6 %subtract_select_fusion = f32[768,12,512]{2,0,1:T(8,128)} fusion(f32[768,12,512]{2,0,1:T(8,128)} %copy-done.2, pred[12]{0:T(512)(128)(4,1)S(1)} %broadcast_compare_fusion.3, f32[12,512,2048]{2,1,0:T(8,128)} %all-gather.2.cloned.1.call-done, f32[768,512]{0,1:T(8,128)S(1)} %copy-done.5), kind=kOutput, calls=%fused_computation.8 | convolution fusion | flops 29000466432 | bytes 51904524 | tf_op jit(solution)/shard_map/ms,lts->mlt/dot_general | solution.py:34
  (88 shorter events, 26.9 us)
Async XLA Ops:
  7.2 302.2 %all-gather.2.cloned.1.call-start = ((), (), s32[]{:S(2)}) async-start(), calls=%async_computation | async-start | bytes 62914560 | tf_op jit(solution)/shard_map/all_gather | solution.py:22
  7.9 456.6 %all-reduce.5.cloned.1.call-start = ((), (), s32[]{:S(2)}) async-start(), calls=%async_computation.1 | async-start | bytes 3145728 | tf_op jit(solution)/shard_map/psum | solution.py:11
  374.8 258.3 %all-reduce.7.cloned.1.call-start = ((), (), s32[]{:S(2)}) async-start(), calls=%async_computation.2 | async-start | bytes 3145728 | tf_op jit(solution)/shard_map/psum | solution.py:11
  533.2 9.2 copy-start.1
  544.2 257.5 %all-reduce.9.cloned.1.call-start = ((), (), s32[]{:S(2)}) async-start(), calls=%async_computation.3 | async-start | bytes 3145728 | tf_op jit(solution)/shard_map/psum | solution.py:11
  702.0 9.2 copy-start
  713.1 254.9 %all-reduce.11.cloned.1.call-start = ((), (), s32[]{:S(2)}) async-start(), calls=%async_computation.4 | async-start | bytes 3145728 | tf_op jit(solution)/shard_map/psum | solution.py:11
  870.7 6.9 copy-start.2
  878.0 89.9 %copy-start.4 = (f32[768,512]{0,1:T(8,128)S(1)}, f32[768,512]{0,1:T(8,128)}, u32[]{:S(2)}) copy-start(f32[768,512]{0,1:T(8,128)} %all-reduce.7.cloned.1.call-done) | copy-start | bytes 4718596
  879.3 88.7 %copy-start.3 = (f32[768,512]{0,1:T(8,128)S(1)}, f32[768,512]{0,1:T(8,128)}, u32[]{:S(2)}) copy-start(f32[768,512]{0,1:T(8,128)} %all-reduce.5.cloned.1.call-done) | copy-start | bytes 4718596
  973.0 6.7 copy-start.5
Sparse Core Ops, SparseCore 0:
  9.5 299.8 all-gather.1
  374.9 89.4 all-reduce.4
  544.3 88.7 all-reduce.6
  713.2 88.5 all-reduce.8
  879.4 88.4 all-reduce.10
where the time goes:
time: 1060 us; the launch traced here: 1050 us
  waiting for transfers between devices  507 us (48%)
  matrix products  309 us (29%)
  other arithmetic  171 us (16%)
  local copies, waits for them, and re-layouts  52.2 us (5%)
  between operations  14.4 us (1%)
    all_gather x1, waiting for transfers between devices, local(): columns = lax.all_gather(factor, 'row', axis=2, tiled=True)  300 us
    dot_general x4, matrix products, local(): jnp.einsum('ms,lts->mlt', solved_block, part_cols, precision=lax.Precisio...  274 us
    psum x4, waiting for transfers between devices, from_root(): return lax.psum(kept, axis)  206 us
    another operation x6, other arithmetic, local(): lax.linalg.triangular_solve(guarded, current[:, local_block, :], left_sid...  161 us
    another operation x53, local copies, waits for them, and re-layouts, local(): lax.linalg.triangular_solve(guarded, current[:, local_block, :], left_sid...  42.9 us
    another operation x28, matrix products, local(): lax.linalg.triangular_solve(guarded, current[:, local_block, :], left_sid...  34.7 us
  transfers between devices with their start and end apart: 5, of which 5 were waited for; matrix products, arithmetic and copies ran while one was open for 14% of the time, Pallas kernels for 0%

commit v1 on v0

--- a/solution.py
+++ b/solution.py
@@ -8,7 +8,7 @@
 
 def from_root(value, axis, source):
     kept = jnp.where(lax.axis_index(axis) == source, value, 0).astype(value.dtype)
-    return lax.psum(kept, axis)
+    return jnp.sum(lax.all_gather(kept, axis), axis=0)
 
 
 def local(matrix, factor):

time: 1060 us -> 1500 us (1.42)
  waiting for transfers between devices: 507 us -> 851 us
  local copies, waits for them, and re-layouts: 52.2 us -> 111 us
  other arithmetic: 171 us -> 203 us
    all_gather x0 -> x4, waiting for transfers between devices: none -> 550 us  [from_root(): return jnp.sum(lax.all_gather(kept, axis), axis=0)]
    psum x4 -> x0, waiting for transfers between devices: 206 us -> none  [from_root(): return lax.psum(kept, axis)]
    unnamed x13 -> x21, local copies, waits for them, and re-layouts: 7.45 us -> 67.7 us
    reduce_sum x0 -> x4, other arithmetic: none -> 31.9 us  [from_root(): return jnp.sum(lax.all_gather(kept, axis), axis=0)]
  transfers between devices with their start and end apart: 5 -> 5, of which waited for: 5 -> 5; matrix products, arithmetic and copies ran while one was open for 14% -> 10% of each run, Pallas kernels for 0% -> 0%
where the time goes in v1:
time: 1500 us; the launch traced here: 1490 us
  waiting for transfers between devices  851 us (57%)
  matrix products  315 us (21%)
  other arithmetic  203 us (14%)
  local copies, waits for them, and re-layouts  111 us (7%)
    all_gather x4, waiting for transfers between devices, from_root(): return jnp.sum(lax.all_gather(kept, axis), axis=0)  550 us
    all_gather x1, waiting for transfers between devices, local(): columns = lax.all_gather(factor, 'row', axis=2, tiled=True)  300 us
    dot_general x4, matrix products, local(): jnp.einsum('ms,lts->mlt', solved_block, part_cols, precision=lax.Precisio...  277 us
    another operation x6, other arithmetic, local(): lax.linalg.triangular_solve(guarded, current[:, local_block, :], left_sid...  162 us
    unnamed x21, local copies, waits for them, and re-layouts  67.7 us
    another operation x53, local copies, waits for them, and re-layouts, local(): lax.linalg.triangular_solve(guarded, current[:, local_block, :], left_sid...  41.5 us
    another operation x28, matrix products, local(): lax.linalg.triangular_solve(guarded, current[:, local_block, :], left_sid...  37.6 us
    reduce_sum x4, other arithmetic, from_root(): return jnp.sum(lax.all_gather(kept, axis), axis=0)  31.9 us
  transfers between devices with their start and end apart: 5, of which 5 were waited for; matrix products, arithmetic and copies ran while one was open for 10% of the time, Pallas kernels for 0%

profile of v1, /device:TPU:0, one launch (start us, length us, event | category | flops | bytes accessed | tf_op | source)
XLA Modules:
  0.0 1494.9 jit_solution(8317419061509424902)
XLA Ops:
  9.5 299.9 %all-gather.10.cloned.1.call-done = f32[12,512,2048]{2,1,0:T(8,128)} async-done(((f32[12,512,512]{2,1,0:T(8,128)}), f32[12,512,2048]{2,1,0:T(8,128)}) %all-gather.10.cloned.1.call-update) | async-done | bytes 50331664 | tf_op jit(solution)/shard_map/all_gather | solution.py:22
  309.4 4.2 fusion.43
  313.6 11.3 while.8
  314.2 2.2 bitcast_dynamic-update-slice_fusion.8
  317.1 2.2 bitcast_dynamic-update-slice_fusion.8
  319.9 2.2 bitcast_dynamic-update-slice_fusion.8
  322.7 2.1 bitcast_dynamic-update-slice_fusion.8
  324.9 39.3 %custom-call.6 = f32[4,128,128]{1,2,0:T(8,128)S(1)} custom-call(f32[4,128,128]{2,1,0:T(8,128)S(1)} %get-tuple-element.29), custom_call_target="InvertDiagBlocksLowerTriangular" | custom-call | tf_op jit(solution)/shard_map/triangular_solve/custom-call.1 | solution.py:29
  366.9 2.3 convolution_subtract_fusion.11
  369.8 3.1 convolution_subtract_fusion.6
  374.9 11.4 while.9
  375.6 2.2 bitcast_dynamic-update-slice_fusion.9
  378.4 2.2 bitcast_dynamic-update-slice_fusion.9
  381.2 2.3 bitcast_dynamic-update-slice_fusion.9
  384.1 2.2 bitcast_dynamic-update-slice_fusion.9
  386.3 39.3 %custom-call.7 = f32[4,128,128]{1,2,0:T(8,128)S(1)} custom-call(f32[4,128,128]{2,1,0:T(8,128)S(1)} %get-tuple-element.30), custom_call_target="InvertDiagBlocksLowerTriangular" | custom-call | tf_op jit(solution)/shard_map/triangular_solve/custom-call.1 | solution.py:29
  425.6 125.3 %all-gather.12.cloned.1.call-done = f32[6144,512]{0,1:T(8,128)} async-done(((f32[768,512]{0,1:T(8,128)}), f32[6144,512]{0,1:T(8,128)}) %all-gather.12.cloned.1.call-update) | async-done | bytes 12582928 | tf_op jit(solution)/shard_map/all_gather | solution.py:11
  550.9 15.2 %copy.17 = f32[64,8,8,768]{3,2,1,0:T(8,128)} copy(f32[64,8,8,768]{3,1,2,0:T(8,128)} %bitcast.165) | data formatting | bytes 25165824
  566.1 7.6 bitcast_reduce_fusion.3
  573.7 69.4 %subtract_select_fusion.3 = f32[768,12,512]{2,0,1:T(8,128)S(1)} fusion(f32[768,12,512]{2,0,1:T(8,128)} %param.4, pred[12]{0:T(512)(128)(4,1)S(1)} %broadcast_compare_fusion, f32[12,512,2048]{2,1,0:T(8,128)} %all-gather.10.cloned.1.call-done, f32[768,512]{0,1:T(8,128)S(1)} %bitcast_reduce_fusion.3), kind=kOutput, calls=%fused_computation.11 | convolution fusion | flops 29000466432 | bytes 51904524 | tf_op jit(solution)/shard_map/ms,lts->mlt/dot_general | solution.py:34
  646.0 2.5 convolution_subtract_fusion.10
  649.0 3.3 convolution_subtract_fusion.4
  654.2 7.7 while.10
  662.0 39.3 %custom-call.8 = f32[4,128,128]{1,2,0:T(8,128)S(1)} custom-call(f32[4,128,128]{2,1,0:T(8,128)S(1)} %get-tuple-element.31), custom_call_target="InvertDiagBlocksLowerTriangular" | custom-call | tf_op jit(solution)/shard_map/triangular_solve/custom-call.1 | solution.py:29
  701.3 127.3 %all-gather.14.cloned.1.call-done = f32[6144,512]{0,1:T(8,128)} async-done(((f32[768,512]{0,1:T(8,128)}), f32[6144,512]{0,1:T(8,128)}) %all-gather.14.cloned.1.call-update) | async-done | bytes 12582928 | tf_op jit(solution)/shard_map/all_gather | solution.py:11
  828.6 14.9 copy.18
  843.5 7.6 bitcast_reduce_fusion.2
  851.1 69.4 %subtract_select_fusion.2 = f32[768,12,512]{2,0,1:T(8,128)S(1)} fusion(f32[768,12,512]{2,0,1:T(8,128)} %copy-done.1, pred[12]{0:T(512)(128)(4,1)S(1)} %broadcast_compare_fusion.1, f32[12,512,2048]{2,1,0:T(8,128)} %all-gather.10.cloned.1.call-done, f32[768,512]{0,1:T(8,128)S(1)} %bitcast_reduce_fusion.2), kind=kOutput, calls=%fused_computation.10 | convolution fusion | flops 29000466432 | bytes 51904524 | tf_op jit(solution)/shard_map/ms,lts->mlt/dot_general | solution.py:34
  923.4 2.5 convolution_subtract_fusion.9
  926.4 3.3 convolution_subtract_fusion.2
  931.6 11.4 while.11
  932.2 2.2 bitcast_dynamic-update-slice_fusion.11
  935.0 2.2 bitcast_dynamic-update-slice_fusion.11
  937.9 2.2 bitcast_dynamic-update-slice_fusion.11
  940.8 2.1 bitcast_dynamic-update-slice_fusion.11
  942.9 39.9 %custom-call.9 = f32[4,128,128]{1,2,0:T(8,128)} custom-call(f32[4,128,128]{2,1,0:T(8,128)S(1)} %get-tuple-element.32), custom_call_target="InvertDiagBlocksLowerTriangular" | custom-call | tf_op jit(solution)/shard_map/triangular_solve/custom-call.1 | solution.py:29
  982.9 123.1 %all-gather.16.cloned.1.call-done = f32[6144,512]{0,1:T(8,128)} async-done(((f32[768,512]{0,1:T(8,128)}), f32[6144,512]{0,1:T(8,128)}) %all-gather.16.cloned.1.call-update) | async-done | bytes 12582928 | tf_op jit(solution)/shard_map/all_gather | solution.py:11
  1105.9 14.9 copy.19
  1120.8 7.9 bitcast_reduce_fusion.1
  1128.8 70.9 %subtract_select_fusion.1 = f32[768,12,512]{2,0,1:T(8,128)S(1)} fusion(f32[768,12,512]{2,0,1:T(8,128)} %copy-done, pred[12]{0:T(512)(128)(4,1)S(1)} %broadcast_compare_fusion.2, f32[12,512,2048]{2,1,0:T(8,128)} %all-gather.10.cloned.1.call-done, f32[768,512]{0,1:T(8,128)S(1)} %bitcast_reduce_fusion.1), kind=kOutput, calls=%fused_computation.9 | convolution fusion | flops 29000466432 | bytes 51904524 | tf_op jit(solution)/shard_map/ms,lts->mlt/dot_general | solution.py:34
  1203.6 2.5 convolution_subtract_fusion.8
  1206.6 3.1 convolution_subtract_fusion
  1211.5 174.4 %all-gather.18.cloned.1.call-done = f32[6144,512]{0,1:T(8,128)} async-done(((f32[768,512]{0,1:T(8,128)}), f32[6144,512]{0,1:T(8,128)}) %all-gather.18.cloned.1.call-update) | async-done | bytes 12582928 | tf_op jit(solution)/shard_map/all_gather | solution.py:11
  1385.9 15.1 %copy.20 = f32[64,8,8,768]{3,2,1,0:T(8,128)} copy(f32[64,8,8,768]{3,1,2,0:T(8,128)} %bitcast.167) | data formatting | bytes 25165824
  1401.0 8.8 bitcast_reduce_fusion
  1409.8 4.1 pad_maximum_fusion
  1413.9 6.7 copy.8
  1420.6 67.4 %subtract_select_fusion = f32[768,12,512]{2,0,1:T(8,128)} fusion(f32[768,12,512]{2,0,1:T(8,128)} %copy-done.2, pred[12]{0:T(512)(128)(4,1)S(1)} %broadcast_compare_fusion.3, f32[12,512,2048]{2,1,0:T(8,128)} %all-gather.10.cloned.1.call-done, f32[768,512]{0,1:T(8,128)S(1)} %copy-done.5), kind=kOutput, calls=%fused_computation.8 | convolution fusion | flops 29000466432 | bytes 51904524 | tf_op jit(solution)/shard_map/ms,lts->mlt/dot_general | solution.py:34
  (100 shorter events, 39.4 us)
Async XLA Ops:
  7.2 302.2 %all-gather.10.cloned.1.call-start = ((), (), s32[]{:S(2)}) async-start(), calls=%async_computation | async-start | bytes 62914560 | tf_op jit(solution)/shard_map/all_gather | solution.py:22
  7.9 543.0 %all-gather.12.cloned.1.call-start = ((), (), s32[]{:S(2)}) async-start(), calls=%async_computation.1 | async-start | bytes 14155776 | tf_op jit(solution)/shard_map/all_gather | solution.py:11
  374.7 453.9 %all-gather.14.cloned.1.call-start = ((), (), s32[]{:S(2)}) async-start(), calls=%async_computation.2 | async-start | bytes 14155776 | tf_op jit(solution)/shard_map/all_gather | solution.py:11
  643.1 9.2 copy-start.1
  654.1 451.8 %all-gather.16.cloned.1.call-start = ((), (), s32[]{:S(2)}) async-start(), calls=%async_computation.3 | async-start | bytes 14155776 | tf_op jit(solution)/shard_map/all_gather | solution.py:11
  662.0 166.7 %copy-start.6 = (f32[512,512]{1,0:T(8,128)}, f32[512,512]{1,0:T(8,128)S(1)}, u32[]{:S(2)}) copy-start(f32[512,512]{1,0:T(8,128)S(1)} %get-tuple-element.276) | copy-start | bytes 3145732
  920.4 9.2 copy-start
  931.5 454.4 %all-gather.18.cloned.1.call-start = ((), (), s32[]{:S(2)}) async-start(), calls=%async_computation.4 | async-start | bytes 14155776 | tf_op jit(solution)/shard_map/all_gather | solution.py:11
  1128.7 70.9 %copy-start.3 = (f32[768,512]{0,1:T(8,128)}, f32[768,512]{0,1:T(8,128)S(1)}, u32[]{:S(2)}) copy-start(f32[768,512]{0,1:T(8,128)S(1)} %bitcast_reduce_fusion.1) | copy-start | bytes 4718596
  1199.6 10.0 copy-start.2
  1199.6 1.1 copy-start.7
  1401.0 8.8 copy-start.4
  1413.9 6.7 copy-start.5
Sparse Core Ops, SparseCore 0:
  9.5 299.8 all-gather.9
  374.8 176.0 all-gather.11
  654.2 174.3 all-gather.13
  931.6 174.2 all-gather.15
  1211.6 174.2 all-gather.17
